TPU v7x, 32 devices: a whole 2x2x4 slice. The times are simulated.
32 devices in a mesh: sx: 4 (over x, core), sy: 2 (over y), px: 4 (over z).
Axes of the slice: x: 2, y: 2, z: 4, core: 2. Of those that a mesh axis runs over, the one named last changes fastest.
Arguments:
- patterns: bfloat16 [64, 64, 9216], P('sx', 'sy', 'px'), may hold values from -6 to 6
- basis: bfloat16 [9216, 256], P('px', ('sx', 'sy')), may hold values from -0.375 to 0.375
- valid: int32 [64, 64], P('sx', 'sy'), may hold values 0 or 1
- strength: float32 [64, 64], P('sx', 'sy'), may hold values from 0.25 to 2
Outputs:
- denoised: bfloat16 [64, 64, 9216], P('sx', 'sy', 'px')
Inputs may be any that keep to these rules, and one draw needn't show every extreme that they name: `valid`: 1 marks an on-sample scan position, 0 an off-sample one.
All inputs are finite; a program needn't handle non-finite values. No bound on the sum of `valid` on one device may be relied on, other than what follows from the above.
Results may differ from a plain program's by a relative error of at most 0.0089.
Values may be sent and summed in bfloat16 or wider, within the bound.
No kernel may reach another device: no remote copies, remote signals or barrier semaphores. Data moves between devices by JAX's collectives and lax.ppermute only.
A program may use at most 64 MiB of HBM per device.

v0:
```python
import jax
import jax.numpy as jnp
from jax import lax
from jax.sharding import PartitionSpec as P

PIX = 9216
RADIUS = 3


def extended(array, sides, width):
    for axis, dim in sides:
        count, length = (lax.axis_size(axis), array.shape[dim])
        up = [(i, (i + 1) % count) for i in range(count - 1)]
        down = [(j, i) for i, j in up]
        last = lax.slice_in_dim(array, length - width, length, axis=dim)
        initial = lax.slice_in_dim(array, 0, width, axis=dim)
        before = lax.ppermute(last, axis, up)
        after = lax.ppermute(initial, axis, down)
        array = jnp.concatenate([before, array, after], axis=dim)
    return array


def neighbour_steps():
    steps = []
    for row_step in range(-RADIUS, RADIUS + 1):
        for col_step in range(-RADIUS, RADIUS + 1):
            if row_step != 0 or col_step != 0:
                steps.append((row_step, col_step))
    return steps


def squared_gaps(center, padded):
    rows, cols = (center.shape[0], center.shape[1])
    gaps = []
    for row_step, col_step in neighbour_steps():
        other = padded[
            RADIUS + row_step : RADIUS + row_step + rows,
            RADIUS + col_step : RADIUS + col_step + cols,
        ]
        differ = center - other
        gaps.append(jnp.sum(differ * differ, axis=-1))
    return jnp.stack(gaps)


def blend(center, padded, mask_pad, gaps, strength):
    rows, cols = (center.shape[0], center.shape[1])
    factor = 1.0 / (2.0 * PIX * strength)
    numerator = center
    total = jnp.ones((rows, cols), jnp.float32)
    for index, (row_step, col_step) in enumerate(neighbour_steps()):
        other = padded[
            RADIUS + row_step : RADIUS + row_step + rows,
            RADIUS + col_step : RADIUS + col_step + cols,
        ]
        mask_other = mask_pad[
            RADIUS + row_step : RADIUS + row_step + rows,
            RADIUS + col_step : RADIUS + col_step + cols,
        ]
        weight = mask_other * jnp.exp(-gaps[index] * factor)
        numerator = numerator + weight[:, :, None] * other
        total = total + weight
    return numerator / total[:, :, None]


def extend(coeffs, mask_full):
    return (
        extended(coeffs, (("sx", 0), ("sy", 1)), RADIUS),
        extended(mask_full, (("sx", 0), ("sy", 1)), RADIUS),
    )


def on_device(patterns, basis, valid, strength):
    cells_x, cells_y, pixels = patterns.shape
    flat = patterns.reshape(cells_x * cells_y, pixels)
    whole_basis = lax.all_gather(basis, ("sx", "sy"), axis=1, tiled=True)
    partial_value = jnp.dot(flat, whole_basis, preferred_element_type=jnp.float32)
    partial_value = partial_value.reshape(cells_x, cells_y, partial_value.shape[1])
    mask_full = valid.astype(jnp.float32)
    coeffs = lax.psum(partial_value, "px")
    padded, mask_pad = extend(coeffs, mask_full)
    gaps = squared_gaps(coeffs, padded)
    average = blend(coeffs, padded, mask_pad, gaps, strength).astype(jnp.bfloat16)
    avg_flat = average.reshape(cells_x * cells_y, average.shape[2])
    rebuilt = lax.dot_general(
        avg_flat, whole_basis, (((1,), (1,)), ((), ())), preferred_element_type=jnp.float32
    )
    return rebuilt.astype(jnp.bfloat16).reshape(cells_x, cells_y, pixels)


def solution(mesh):
    return jax.shard_map(
        on_device,
        mesh=mesh,
        in_specs=(P("sx", "sy", "px"), P("px", ("sx", "sy")), P("sx", "sy"), P("sx", "sy")),
        out_specs=P("sx", "sy", "px"),
        check_vma=False,
    )
```

profile of v0, /device:TPU:1, one launch (start us, length us, event | category | flops | bytes accessed | tf_op | source)
XLA Modules:
  0.0 117.6 jit_solution(7627593339896749223)
XLA Ops:
  6.5 0.0 copy-start
  6.5 0.0 all-gather.2.cloned.1.call-start
  6.5 0.7 all-gather.2.cloned.1.call-update
  7.3 0.0 copy-start.4
  7.3 0.0 all-reduce.2.cloned.1.call-start
  7.3 28.3 %all-gather.2.cloned.1.call-done = bf16[2304,256]{0,1:T(8,128)(2,1)} async-done(((bf16[2304,32]{0,1:T(8,128)(2,1)}), bf16[2304,256]{0,1:T(8,128)(2,1)}) %all-gather.2.cloned.1.call-update) | async-done | bytes 1179664 | tf_op jit(solution)/shard_map/all_gather | solution.py:75
  35.6 0.0 copy-done
  35.6 2.9 %fusion = f32[16,32,256]{2,1,0:T(8,128)} fusion(bf16[16,32,2304]{2,1,0:T(8,128)(2,1)S(1)} %copy-done, bf16[2304,256]{0,1:T(8,128)(2,1)} %all-gather.2.cloned.1.call-done), kind=kOutput, calls=%fused_computation.81 | convolution fusion | flops 603979776 | bytes 4063232 | tf_op jit(solution)/shard_map/dot_general | solution.py:76
  38.5 0.0 all-reduce.2.cloned.1.call-update
  38.5 0.0 copy-done.4
  38.6 3.3 %collective-permute-start = (f32[3,32]{1,0:T(4,128)S(1)}, f32[3,32]{1,0:T(4,128)S(1)}, u32[]{:S(2)}, u32[]{:S(2)}) collective-permute-start(f32[3,32]{1,0:T(4,128)S(1)} %get-tuple-element.124), channel_id=1, source_target_pairs={{0,8},{8,16},{16,24},{1,9},{9,17},{17,25},{2,10},{10,18},{18,26},{... | collective-permute-start | bytes 1160 | tf_op jit(solution)/shard_map/ppermute | solution.py:17
  41.8 1.9 %collective-permute-start.1 = (f32[3,32]{1,0:T(4,128)S(1)}, f32[3,32]{1,0:T(4,128)S(1)}, u32[]{:S(2)}, u32[]{:S(2)}) collective-permute-start(f32[3,32]{1,0:T(4,128)S(1)} %get-tuple-element.125), channel_id=1, source_target_pairs={{8,0},{16,8},{24,16},{9,1},{17,9},{25,17},{10,2},{18,10},{26,18},{... | collective-permute-start | bytes 1160 | tf_op jit(solution)/shard_map/ppermute | solution.py:18
  43.8 0.0 collective-permute-done
  43.8 3.4 %collective-permute-done.1 = f32[3,32]{1,0:T(4,128)S(1)} collective-permute-done((f32[3,32]{1,0:T(4,128)S(1)}, f32[3,32]{1,0:T(4,128)S(1)}, u32[]{:S(2)}, u32[]{:S(2)}) %collective-permute-start.1) | collective-permute-done | bytes 416 | tf_op jit(solution)/shard_map/ppermute | solution.py:18
  47.1 28.8 %all-reduce.2.cloned.1.call-done = f32[16,32,256]{2,1,0:T(8,128)} async-done(((f32[16,32,256]{2,1,0:T(8,128)}), f32[16,32,256]{2,1,0:T(8,128)}) %all-reduce.2.cloned.1.call-update) | async-done | bytes 524304 | tf_op jit(solution)/shard_map/psum | solution.py:79
  76.0 0.0 copy-start.1
  76.0 1.0 fusion.59
  77.0 4.6 %collective-permute-start.3 = (f32[3,32,256]{2,1,0:T(8,128)S(1)}, f32[3,32,256]{2,1,0:T(8,128)S(1)}, u32[]{:S(2)}, u32[]{:S(2)}) collective-permute-start(f32[3,32,256]{2,1,0:T(8,128)S(1)} %get-tuple-element.116), channel_id=1, source_target_pairs={{0,8},{8,16},{16,24},{1,9},{9,17},{17,25},{2,10},{10,18},{18,26},{... | collective-permute-start | bytes 294920 | tf_op jit(solution)/shard_map/ppermute | solution.py:17
  81.6 0.1 fusion.60
  81.7 3.1 %collective-permute-start.2 = (f32[22,3]{1,0:T(8,128)S(1)}, f32[22,3]{1,0:T(8,128)S(1)}, u32[]{:S(2)}, u32[]{:S(2)}) collective-permute-start(f32[22,3]{1,0:T(8,128)S(1)} %get-tuple-element.123), channel_id=1, source_target_pairs={{0,4},{1,5},{2,6},{3,7},{8,12},{9,13},{10,14},{11,15},{16,20},{17,... | collective-permute-start | bytes 800 | tf_op jit(solution)/shard_map/ppermute | solution.py:17
  84.7 1.3 %collective-permute-start.6 = (f32[22,3]{1,0:T(8,128)S(1)}, f32[22,3]{1,0:T(8,128)S(1)}, u32[]{:S(2)}, u32[]{:S(2)}) collective-permute-start(f32[22,3]{1,0:T(8,128)S(1)} %get-tuple-element.122), channel_id=1, source_target_pairs={{4,0},{5,1},{6,2},{7,3},{12,8},{13,9},{14,10},{15,11},{20,16},{21,... | collective-permute-start | bytes 800 | tf_op jit(solution)/shard_map/ppermute | solution.py:18
  86.0 1.9 %collective-permute-start.4 = (f32[3,32,256]{2,1,0:T(8,128)S(1)}, f32[3,32,256]{2,1,0:T(8,128)S(1)}, u32[]{:S(2)}, u32[]{:S(2)}) collective-permute-start(f32[3,32,256]{2,1,0:T(8,128)S(1)} %get-tuple-element.117), channel_id=1, source_target_pairs={{8,0},{16,8},{24,16},{9,1},{17,9},{25,17},{10,2},{18,10},{26,18},{... | collective-permute-start | bytes 294920 | tf_op jit(solution)/shard_map/ppermute | solution.py:18
  88.0 0.0 collective-permute-done.3
  88.0 1.2 constant_dynamic-update-slice_fusion.1
  89.2 2.8 %collective-permute-done.4 = f32[3,32,256]{2,1,0:T(8,128)S(1)} collective-permute-done((f32[3,32,256]{2,1,0:T(8,128)S(1)}, f32[3,32,256]{2,1,0:T(8,128)S(1)}, u32[]{:S(2)}, u32[]{:S(2)}) %collective-permute-start.4) | collective-permute-done | bytes 98336 | tf_op jit(solution)/shard_map/ppermute | solution.py:18
  92.0 1.3 %collective-permute-start.7 = (f32[22,3,256]{2,1,0:T(4,128)S(1)}, f32[22,3,256]{2,1,0:T(4,128)S(1)}, u32[]{:S(2)}, u32[]{:S(2)}) collective-permute-start(f32[22,3,256]{2,1,0:T(4,128)S(1)} %get-tuple-element.111), channel_id=1, source_target_pairs={{4,0},{5,1},{6,2},{7,3},{12,8},{13,9},{14,10},{15,11},{20,16},{21,... | collective-permute-start | bytes 202760 | tf_op jit(solution)/shard_map/ppermute | solution.py:18
  93.3 0.0 collective-permute-done.2
  93.3 0.0 collective-permute-done.6
  93.4 0.1 pad_maximum_fusion.3
  93.4 4.0 %collective-permute-start.5 = (f32[22,3,256]{2,1,0:T(4,128)S(1)}, f32[22,3,256]{2,1,0:T(4,128)S(1)}, u32[]{:S(2)}, u32[]{:S(2)}) collective-permute-start(f32[22,3,256]{2,1,0:T(4,128)S(1)} %get-tuple-element.112), channel_id=1, source_target_pairs={{0,4},{1,5},{2,6},{3,7},{8,12},{9,13},{10,14},{11,15},{16,20},{17,... | collective-permute-start | bytes 202760 | tf_op jit(solution)/shard_map/ppermute | solution.py:17
  97.4 0.0 collective-permute-done.7
  97.4 0.0 copy-done.1
  97.4 1.0 multiply_reduce_fusion.42
  98.4 1.0 multiply_reduce_fusion.43
  99.4 0.0 collective-permute-done.5
  99.4 1.1 multiply_reduce_fusion.46
  100.6 1.1 multiply_reduce_fusion.47
  101.7 0.0 copy-start.3
  101.7 1.2 %multiply_reduce_fusion.45 = (f32[16,32]{1,0:T(8,128)S(1)}, f32[16,32]{1,0:T(8,128)S(1)}, f32[16,32]{1,0:T(8,128)S(1)}, f32[16,32]{1,0:T(8,128)S(1)}, f32[16,32]...) fusion(f32[16,32,256]{2,1,0:T(8,128)S(1)} %copy-done.1, ...), kind=kLoop, calls=%fused_computation.171 | loop fusion | flops 5498880 | bytes 4550656 | tf_op jit(solution)/shard_map/reduce_sum | solution.py:41
  102.9 0.0 copy-done.3
  102.9 0.2 add_add_fusion
  103.1 0.0 copy-start.2
  103.1 5.4 %divide_convert_fusion = bf16[16,32,256]{2,1,0:T(8,128)(2,1)S(1)} fusion(f32[16,32,256]{2,1,0:T(8,128)S(1)} %copy-done.1, f32[19,32,256]{2,1,0:T(8,128)S(1)} %constant_dynamic-update-slice_fusion.5, f32[19,32,256]{2,1,0:T(8,128)S(1)} %get-tuple-element.115, f32[22,32,256]{2,1,0:T(8,128)S(1)} %constant_dynamic-update-slice_fusion, ...), kind=kLoop, calls=%fused_computation.125 | loop fusion | flops 18350080 | bytes 4888576 | tf_op jit(solution)/shard_map/convert_element_type | solution.py:82
  108.6 0.0 copy-done.2
  108.6 2.2 %convolution_convert_fusion = bf16[512,2304]{1,0:T(8,128)(2,1)} fusion(bf16[512,256]{1,0:T(8,128)(2,1)S(1)} %bitcast.8, bf16[2304,256]{0,1:T(8,128)(2,1)S(1)} %copy-done.2), kind=kOutput, calls=%fused_computation.40 | convolution fusion | flops 605159424 | bytes 3801088 | tf_op jit(solution)/shard_map/dot_general | solution.py:84
  (7 shorter events, 0.1 us)
Async XLA Ops:
  6.5 29.1 %copy-start = (bf16[16,32,2304]{2,1,0:T(8,128)(2,1)S(1)}, bf16[16,32,2304]{2,1,0:T(8,128)(2,1)}, u32[]{:S(2)}) copy-start(bf16[16,32,2304]{2,1,0:T(8,128)(2,1)} %param.4) | copy-start | bytes 7077892
  6.5 29.1 %all-gather.2.cloned.1.call-start = ((), (), s32[]{:S(2)}) async-start(), calls=%async_computation | async-start | bytes 1327104 | tf_op jit(solution)/shard_map/all_gather | solution.py:75
  7.3 31.3 %copy-start.4 = (s32[16,32]{1,0:T(8,128)S(1)}, s32[16,32]{1,0:T(8,128)}, u32[]{:S(2)}) copy-start(s32[16,32]{1,0:T(8,128)} %param.6) | copy-start | bytes 6148
  7.3 68.7 %all-reduce.2.cloned.1.call-start = ((), (), s32[]{:S(2)}) async-start(), calls=%async_computation.1 | async-start | bytes 1048576 | tf_op jit(solution)/shard_map/psum | solution.py:79
  38.6 5.2 %collective-permute-start = (f32[3,32]{1,0:T(4,128)S(1)}, f32[3,32]{1,0:T(4,128)S(1)}, u32[]{:S(2)}, u32[]{:S(2)}) collective-permute-start(f32[3,32]{1,0:T(4,128)S(1)} %get-tuple-element.124), channel_id=1, source_target_pairs={{0,8},{8,16},{16,24},{1,9},{9,17},{17,25},{2,10},{10,18},{18,26},{... | collective-permute-start | bytes 1160 | tf_op jit(solution)/shard_map/ppermute | solution.py:17
  41.8 5.3 %collective-permute-start.1 = (f32[3,32]{1,0:T(4,128)S(1)}, f32[3,32]{1,0:T(4,128)S(1)}, u32[]{:S(2)}, u32[]{:S(2)}) collective-permute-start(f32[3,32]{1,0:T(4,128)S(1)} %get-tuple-element.125), channel_id=1, source_target_pairs={{8,0},{16,8},{24,16},{9,1},{17,9},{25,17},{10,2},{18,10},{26,18},{... | collective-permute-start | bytes 1160 | tf_op jit(solution)/shard_map/ppermute | solution.py:18
  76.0 21.5 %copy-start.1 = (f32[16,32,256]{2,1,0:T(8,128)S(1)}, f32[16,32,256]{2,1,0:T(8,128)}, u32[]{:S(2)}) copy-start(f32[16,32,256]{2,1,0:T(8,128)} %all-reduce.2.cloned.1.call-done) | copy-start | bytes 1572868
  77.0 11.0 %collective-permute-start.3 = (f32[3,32,256]{2,1,0:T(8,128)S(1)}, f32[3,32,256]{2,1,0:T(8,128)S(1)}, u32[]{:S(2)}, u32[]{:S(2)}) collective-permute-start(f32[3,32,256]{2,1,0:T(8,128)S(1)} %get-tuple-element.116), channel_id=1, source_target_pairs={{0,8},{8,16},{16,24},{1,9},{9,17},{17,25},{2,10},{10,18},{18,26},{... | collective-permute-start | bytes 294920 | tf_op jit(solution)/shard_map/ppermute | solution.py:17
  81.7 11.7 %collective-permute-start.2 = (f32[22,3]{1,0:T(8,128)S(1)}, f32[22,3]{1,0:T(8,128)S(1)}, u32[]{:S(2)}, u32[]{:S(2)}) collective-permute-start(f32[22,3]{1,0:T(8,128)S(1)} %get-tuple-element.123), channel_id=1, source_target_pairs={{0,4},{1,5},{2,6},{3,7},{8,12},{9,13},{10,14},{11,15},{16,20},{17,... | collective-permute-start | bytes 800 | tf_op jit(solution)/shard_map/ppermute | solution.py:17
  84.7 8.6 %collective-permute-start.6 = (f32[22,3]{1,0:T(8,128)S(1)}, f32[22,3]{1,0:T(8,128)S(1)}, u32[]{:S(2)}, u32[]{:S(2)}) collective-permute-start(f32[22,3]{1,0:T(8,128)S(1)} %get-tuple-element.122), channel_id=1, source_target_pairs={{4,0},{5,1},{6,2},{7,3},{12,8},{13,9},{14,10},{15,11},{20,16},{21,... | collective-permute-start | bytes 800 | tf_op jit(solution)/shard_map/ppermute | solution.py:18
  86.0 5.9 %collective-permute-start.4 = (f32[3,32,256]{2,1,0:T(8,128)S(1)}, f32[3,32,256]{2,1,0:T(8,128)S(1)}, u32[]{:S(2)}, u32[]{:S(2)}) collective-permute-start(f32[3,32,256]{2,1,0:T(8,128)S(1)} %get-tuple-element.117), channel_id=1, source_target_pairs={{8,0},{16,8},{24,16},{9,1},{17,9},{25,17},{10,2},{18,10},{26,18},{... | collective-permute-start | bytes 294920 | tf_op jit(solution)/shard_map/ppermute | solution.py:18
  92.0 5.4 %collective-permute-start.7 = (f32[22,3,256]{2,1,0:T(4,128)S(1)}, f32[22,3,256]{2,1,0:T(4,128)S(1)}, u32[]{:S(2)}, u32[]{:S(2)}) collective-permute-start(f32[22,3,256]{2,1,0:T(4,128)S(1)} %get-tuple-element.111), channel_id=1, source_target_pairs={{4,0},{5,1},{6,2},{7,3},{12,8},{13,9},{14,10},{15,11},{20,16},{21,... | collective-permute-start | bytes 202760 | tf_op jit(solution)/shard_map/ppermute | solution.py:18
  93.4 6.0 %collective-permute-start.5 = (f32[22,3,256]{2,1,0:T(4,128)S(1)}, f32[22,3,256]{2,1,0:T(4,128)S(1)}, u32[]{:S(2)}, u32[]{:S(2)}) collective-permute-start(f32[22,3,256]{2,1,0:T(4,128)S(1)} %get-tuple-element.112), channel_id=1, source_target_pairs={{0,4},{1,5},{2,6},{3,7},{8,12},{9,13},{10,14},{11,15},{16,20},{17,... | collective-permute-start | bytes 202760 | tf_op jit(solution)/shard_map/ppermute | solution.py:17
  101.7 1.2 %copy-start.3 = (f32[16,32]{1,0:T(8,128)S(1)}, f32[16,32]{1,0:T(8,128)}, u32[]{:S(2)}) copy-start(f32[16,32]{1,0:T(8,128)} %param.7) | copy-start | bytes 6148
  103.1 5.5 %copy-start.2 = (bf16[2304,256]{0,1:T(8,128)(2,1)S(1)}, bf16[2304,256]{0,1:T(8,128)(2,1)}, u32[]{:S(2)}) copy-start(bf16[2304,256]{0,1:T(8,128)(2,1)} %all-gather.2.cloned.1.call-done) | copy-start | bytes 3538948
Sparse Core Ops, SparseCore 0:
  9.2 26.3 all-gather.1
  38.6 37.2 all-reduce.1
where the time goes:
time: 118 us
  waiting for transfers between devices  64.1 us (54%)
  starting transfers between devices  21.4 us (18%)
  between operations  13.7 us (12%)
  other arithmetic  11.1 us (9%)
  matrix products  5.06 us (4%)
  local copies, waits for them, and re-layouts  2.33 us (2%)
    psum x1, waiting for transfers between devices, on_device(): coeffs = lax.psum(partial_value, 'px')  28.8 us
    all_gather x1, waiting for transfers between devices, on_device(): whole_basis = lax.all_gather(basis, ('sx', 'sy'), axis=1, tiled=True)  28.3 us
    ppermute x4, starting transfers between devices, extended(): before = lax.ppermute(last, axis, up)  14.9 us
    ppermute x4, starting transfers between devices, extended(): after = lax.ppermute(initial, axis, down)  6.43 us
    ppermute x4, waiting for transfers between devices, extended(): after = lax.ppermute(initial, axis, down)  6.18 us
    convert_element_type x1, other arithmetic, on_device(): blend(coeffs, padded, mask_pad, gaps, strength).astype(jnp.bfloat16)  5.44 us
    reduce_sum x5, other arithmetic, squared_gaps(): gaps.append(jnp.sum(differ * differ, axis=-1))  5.39 us
    dot_general x1, matrix products, on_device(): jnp.dot(flat, whole_basis, preferred_element_type=jnp.float32)  2.87 us
  transfers between devices with their start and end apart: 10, of which 4 were waited for; matrix products, arithmetic and copies ran while one was open for 3% of the time, Pallas kernels for 0%

commit v1 on v0

--- a/solution.py
+++ b/solution.py
@@ -76,7 +76,9 @@
     partial_value = jnp.dot(flat, whole_basis, preferred_element_type=jnp.float32)
     partial_value = partial_value.reshape(cells_x, cells_y, partial_value.shape[1])
     mask_full = valid.astype(jnp.float32)
-    coeffs = lax.psum(partial_value, "px")
+    coeffs = partial_value
+    for hop in (1, 2):
+        coeffs = coeffs + lax.ppermute(coeffs, "px", [(dev, dev ^ hop) for dev in range(4)])
     padded, mask_pad = extend(coeffs, mask_full)
     gaps = squared_gaps(coeffs, padded)
     average = blend(coeffs, padded, mask_pad, gaps, strength).astype(jnp.bfloat16)

time: 118 us -> 115 us (0.975)
  waiting for transfers between devices: 64.1 us -> 61.5 us
  starting transfers between devices: 21.4 us -> 23.9 us
  local copies, waits for them, and re-layouts: 2.33 us -> 0.11 us
    psum x1 -> x0, waiting for transfers between devices: 28.8 us -> none  [on_device(): coeffs = lax.psum(partial_value, 'px')]
    ppermute x0 -> x2, waiting for transfers between devices: none -> 25.6 us  [on_device(): lax.ppermute(coeffs, 'px', [(dev, dev ^ hop) for dev in range(4)])]
    ppermute x0 -> x2, starting transfers between devices: none -> 3.46 us  [on_device(): lax.ppermute(coeffs, 'px', [(dev, dev ^ hop) for dev in range(4)])]
    reduce_sum x5 -> x3, other arithmetic: 5.39 us -> 5.03 us  [squared_gaps(): gaps.append(jnp.sum(differ * differ, axis=-1))]
  transfers between devices with their start and end apart: 10 -> 11, of which waited for: 4 -> 6; matrix products, arithmetic and copies ran while one was open for 3% -> 0% of each run, Pallas kernels for 0% -> 0%
where the time goes in v1:
time: 115 us; the launch traced here: 114 us
  waiting for transfers between devices  61.5 us (53%)
  starting transfers between devices  23.9 us (21%)
  between operations  13.6 us (12%)
  other arithmetic  10.9 us (9%)
  matrix products  4.26 us (4%)
    all_gather x1, waiting for transfers between devices, on_device(): whole_basis = lax.all_gather(basis, ('sx', 'sy'), axis=1, tiled=True)  28.4 us
    ppermute x2, waiting for transfers between devices, on_device(): lax.ppermute(coeffs, 'px', [(dev, dev ^ hop) for dev in range(4)])  25.6 us
    ppermute x4, starting transfers between devices, extended(): before = lax.ppermute(last, axis, up)  14.1 us
    ppermute x4, waiting for transfers between devices, extended(): after = lax.ppermute(initial, axis, down)  6.7 us
    ppermute x4, starting transfers between devices, extended(): after = lax.ppermute(initial, axis, down)  6.42 us
    convert_element_type x1, other arithmetic, on_device(): blend(coeffs, padded, mask_pad, gaps, strength).astype(jnp.bfloat16)  5.27 us
    reduce_sum x3, other arithmetic, squared_gaps(): gaps.append(jnp.sum(differ * differ, axis=-1))  5.03 us
    ppermute x2, starting transfers between devices, on_device(): lax.ppermute(coeffs, 'px', [(dev, dev ^ hop) for dev in range(4)])  3.46 us
  transfers between devices with their start and end apart: 11, of which 6 were waited for; matrix products, arithmetic and copies ran while one was open for 0% of the time, Pallas kernels for 0%

profile of v1, /device:TPU:1, one launch (start us, length us, event | category | flops | bytes accessed | tf_op | source)
XLA Modules:
  0.0 114.4 jit_solution(12512100017574466511)
XLA Ops:
  6.5 0.0 copy-start
  6.5 0.0 all-gather.2.cloned.1.call-start
  6.5 0.7 all-gather.2.cloned.1.call-update
  7.3 0.0 copy-start.3
  7.3 28.4 %all-gather.2.cloned.1.call-done = bf16[2304,256]{0,1:T(8,128)(2,1)} async-done(((bf16[2304,32]{0,1:T(8,128)(2,1)}), bf16[2304,256]{0,1:T(8,128)(2,1)}) %all-gather.2.cloned.1.call-update) | async-done | bytes 1179664 | tf_op jit(solution)/shard_map/all_gather | solution.py:75
  35.6 0.0 copy-done
  35.6 2.1 %fusion = f32[16,32,256]{2,1,0:T(8,128)S(1)} fusion(bf16[16,32,2304]{2,1,0:T(8,128)(2,1)S(1)} %copy-done, bf16[2304,256]{0,1:T(8,128)(2,1)} %all-gather.2.cloned.1.call-done), kind=kOutput, calls=%fused_computation.1 | convolution fusion | flops 603979776 | bytes 4063232 | tf_op jit(solution)/shard_map/dot_general | solution.py:76
  37.7 1.3 %collective-permute-start = (f32[16,32,256]{2,1,0:T(8,128)S(1)}, f32[16,32,256]{2,1,0:T(8,128)S(1)}, u32[]{:S(2)}, u32[]{:S(2)}) collective-permute-start(f32[16,32,256]{2,1,0:T(8,128)S(1)} %fusion), channel_id=1, source_target_pairs={{0,1},{1,0},{2,3},{3,2},{4,5},{5,4},{6,7},{7,6},{8,9},{9,8},{10,11... | collective-permute-start | bytes 1572872 | tf_op jit(solution)/shard_map/ppermute | solution.py:81
  39.0 12.0 %collective-permute-done = f32[16,32,256]{2,1,0:T(8,128)S(1)} collective-permute-done((f32[16,32,256]{2,1,0:T(8,128)S(1)}, f32[16,32,256]{2,1,0:T(8,128)S(1)}, u32[]{:S(2)}, u32[]{:S(2)}) %collective-permute-start) | collective-permute-done | bytes 524320 | tf_op jit(solution)/shard_map/ppermute | solution.py:81
  51.0 0.1 add.291
  51.1 2.2 %collective-permute-start.1 = (f32[16,32,256]{2,1,0:T(8,128)S(1)}, f32[16,32,256]{2,1,0:T(8,128)S(1)}, u32[]{:S(2)}, u32[]{:S(2)}) collective-permute-start(f32[16,32,256]{2,1,0:T(8,128)S(1)} %add.291), channel_id=1, source_target_pairs={{0,2},{1,3},{2,0},{3,1},{4,6},{5,7},{6,4},{7,5},{8,10},{9,11},{10,... | collective-permute-start | bytes 1572872 | tf_op jit(solution)/shard_map/ppermute | solution.py:81
  53.2 0.0 copy-done.3
  53.3 4.4 %collective-permute-start.2 = (f32[3,32]{1,0:T(4,128)S(1)}, f32[3,32]{1,0:T(4,128)S(1)}, u32[]{:S(2)}, u32[]{:S(2)}) collective-permute-start(f32[3,32]{1,0:T(4,128)S(1)} %get-tuple-element.121), channel_id=1, source_target_pairs={{0,8},{8,16},{16,24},{1,9},{9,17},{17,25},{2,10},{10,18},{18,26},{... | collective-permute-start | bytes 1160 | tf_op jit(solution)/shard_map/ppermute | solution.py:17
  57.7 1.9 %collective-permute-start.3 = (f32[3,32]{1,0:T(4,128)S(1)}, f32[3,32]{1,0:T(4,128)S(1)}, u32[]{:S(2)}, u32[]{:S(2)}) collective-permute-start(f32[3,32]{1,0:T(4,128)S(1)} %get-tuple-element.122), channel_id=1, source_target_pairs={{8,0},{16,8},{24,16},{9,1},{17,9},{25,17},{10,2},{18,10},{26,18},{... | collective-permute-start | bytes 1160 | tf_op jit(solution)/shard_map/ppermute | solution.py:18
  59.6 0.0 collective-permute-done.2
  59.6 3.0 %collective-permute-done.3 = f32[3,32]{1,0:T(4,128)S(1)} collective-permute-done((f32[3,32]{1,0:T(4,128)S(1)}, f32[3,32]{1,0:T(4,128)S(1)}, u32[]{:S(2)}, u32[]{:S(2)}) %collective-permute-start.3) | collective-permute-done | bytes 416 | tf_op jit(solution)/shard_map/ppermute | solution.py:18
  62.6 13.6 %collective-permute-done.1 = f32[16,32,256]{2,1,0:T(8,128)S(1)} collective-permute-done((f32[16,32,256]{2,1,0:T(8,128)S(1)}, f32[16,32,256]{2,1,0:T(8,128)S(1)}, u32[]{:S(2)}, u32[]{:S(2)}) %collective-permute-start.1) | collective-permute-done | bytes 524320 | tf_op jit(solution)/shard_map/ppermute | solution.py:81
  76.2 0.1 add.292
  76.3 4.4 %collective-permute-start.5 = (f32[3,32,256]{2,1,0:T(8,128)S(1)}, f32[3,32,256]{2,1,0:T(8,128)S(1)}, u32[]{:S(2)}, u32[]{:S(2)}) collective-permute-start(f32[3,32,256]{2,1,0:T(8,128)S(1)} %get-tuple-element.115), channel_id=1, source_target_pairs={{0,8},{8,16},{16,24},{1,9},{9,17},{17,25},{2,10},{10,18},{18,26},{... | collective-permute-start | bytes 294920 | tf_op jit(solution)/shard_map/ppermute | solution.py:17
  80.7 1.9 %collective-permute-start.6 = (f32[3,32,256]{2,1,0:T(8,128)S(1)}, f32[3,32,256]{2,1,0:T(8,128)S(1)}, u32[]{:S(2)}, u32[]{:S(2)}) collective-permute-start(f32[3,32,256]{2,1,0:T(8,128)S(1)} %get-tuple-element.116), channel_id=1, source_target_pairs={{8,0},{16,8},{24,16},{9,1},{17,9},{25,17},{10,2},{18,10},{26,18},{... | collective-permute-start | bytes 294920 | tf_op jit(solution)/shard_map/ppermute | solution.py:18
  82.6 0.1 fusion.59
  82.7 1.3 %collective-permute-start.8 = (f32[22,3]{1,0:T(8,128)S(1)}, f32[22,3]{1,0:T(8,128)S(1)}, u32[]{:S(2)}, u32[]{:S(2)}) collective-permute-start(f32[22,3]{1,0:T(8,128)S(1)} %get-tuple-element.119), channel_id=1, source_target_pairs={{4,0},{5,1},{6,2},{7,3},{12,8},{13,9},{14,10},{15,11},{20,16},{21,... | collective-permute-start | bytes 800 | tf_op jit(solution)/shard_map/ppermute | solution.py:18
  84.0 4.0 %collective-permute-start.4 = (f32[22,3]{1,0:T(8,128)S(1)}, f32[22,3]{1,0:T(8,128)S(1)}, u32[]{:S(2)}, u32[]{:S(2)}) collective-permute-start(f32[22,3]{1,0:T(8,128)S(1)} %get-tuple-element.120), channel_id=1, source_target_pairs={{0,4},{1,5},{2,6},{3,7},{8,12},{9,13},{10,14},{11,15},{16,20},{17,... | collective-permute-start | bytes 800 | tf_op jit(solution)/shard_map/ppermute | solution.py:17
  88.0 0.0 collective-permute-done.5
  88.0 0.0 collective-permute-done.6
  88.0 1.3 %collective-permute-start.7 = (f32[22,3,256]{2,1,0:T(4,128)S(1)}, f32[22,3,256]{2,1,0:T(4,128)S(1)}, u32[]{:S(2)}, u32[]{:S(2)}) collective-permute-start(f32[22,3,256]{2,1,0:T(4,128)S(1)} %get-tuple-element.113), channel_id=1, source_target_pairs={{0,4},{1,5},{2,6},{3,7},{8,12},{9,13},{10,14},{11,15},{16,20},{17,... | collective-permute-start | bytes 202760 | tf_op jit(solution)/shard_map/ppermute | solution.py:17
  89.3 1.3 %collective-permute-start.9 = (f32[22,3,256]{2,1,0:T(4,128)S(1)}, f32[22,3,256]{2,1,0:T(4,128)S(1)}, u32[]{:S(2)}, u32[]{:S(2)}) collective-permute-start(f32[22,3,256]{2,1,0:T(4,128)S(1)} %get-tuple-element.114), channel_id=1, source_target_pairs={{4,0},{5,1},{6,2},{7,3},{12,8},{13,9},{14,10},{15,11},{20,16},{21,... | collective-permute-start | bytes 202760 | tf_op jit(solution)/shard_map/ppermute | solution.py:18
  90.6 0.0 collective-permute-done.8
  90.6 0.0 collective-permute-done.4
  90.6 0.1 pad_maximum_fusion.7
  90.7 0.1 collective-permute-done.7
  90.9 3.7 %collective-permute-done.9 = f32[22,3,256]{2,1,0:T(4,128)S(1)} collective-permute-done((f32[22,3,256]{2,1,0:T(4,128)S(1)}, f32[22,3,256]{2,1,0:T(4,128)S(1)}, u32[]{:S(2)}, u32[]{:S(2)}) %collective-permute-start.9) | collective-permute-done | bytes 67616 | tf_op jit(solution)/shard_map/ppermute | solution.py:18
  94.6 0.1 maximum_maximum_fusion
  94.7 1.9 %multiply_reduce_fusion.45 = (f32[16,32]{1,0:T(8,128)S(1)}, f32[16,32]{1,0:T(8,128)S(1)}, f32[16,32]{1,0:T(8,128)S(1)}, f32[16,32]{1,0:T(8,128)S(1)}, f32[16,32]...) fusion(f32[16,32,256]{2,1,0:T(8,128)S(1)} %add.292, ...), kind=kLoop, calls=%fused_computation.99 | loop fusion | flops 7068672 | bytes 9998336 | tf_op jit(solution)/shard_map/reduce_sum | solution.py:41
  96.6 2.1 %multiply_reduce_fusion.41 = (f32[16,32]{1,0:T(8,128)S(1)}, f32[16,32]{1,0:T(8,128)S(1)}, f32[16,32]{1,0:T(8,128)S(1)}, f32[16,32]{1,0:T(8,128)S(1)}, f32[16,32]...) fusion(f32[16,32,256]{2,1,0:T(8,128)S(1)} %add.292, ...), kind=kLoop, calls=%fused_computation.95 | loop fusion | flops 7068672 | bytes 9998336 | tf_op jit(solution)/shard_map/reduce_sum | solution.py:41
  98.7 0.0 copy-start.2
  98.7 1.1 multiply_reduce_fusion.44
  99.8 0.0 copy-done.2
  99.8 0.2 add_add_fusion
  100.0 0.0 copy-start.1
  100.0 5.3 %fusion.41 = bf16[16,32,256]{2,1,0:T(8,128)(2,1)S(1)} fusion(f32[3,32,256]{2,1,0:T(8,128)S(1)} %collective-permute-done.6, f32[16,32,256]{2,1,0:T(8,128)S(1)} %add.292, f32[3,32,256]{2,1,0:T(8,128)S(1)} %collective-permute-done.5, f32[22,35,256]{2,1,0:T(8,128)S(1)} %get-tuple-element.112, f32[22,35,256]{2,1,0:T(8,128)S(1)} %get-tuple-element.111, ...), kind=kLoop, calls=%fused_computation.100 | loop fusion | flops 13631488 | bytes 23103488 | tf_op jit(solution)/shard_map/convert_element_type | solution.py:84
  105.3 0.0 copy-done.1
  105.3 2.2 %convolution_convert_fusion = bf16[512,2304]{1,0:T(8,128)(2,1)} fusion(bf16[512,256]{1,0:T(8,128)(2,1)S(1)} %bitcast.8, bf16[2304,256]{0,1:T(8,128)(2,1)S(1)} %copy-done.1), kind=kOutput, calls=%fused_computation | convolution fusion | flops 605159424 | bytes 3801088 | tf_op jit(solution)/shard_map/dot_general | solution.py:86
  (5 shorter events, 0.1 us)
Async XLA Ops:
  6.5 29.1 %copy-start = (bf16[16,32,2304]{2,1,0:T(8,128)(2,1)S(1)}, bf16[16,32,2304]{2,1,0:T(8,128)(2,1)}, u32[]{:S(2)}) copy-start(bf16[16,32,2304]{2,1,0:T(8,128)(2,1)} %param.4) | copy-start | bytes 7077892
  6.5 29.1 %all-gather.2.cloned.1.call-start = ((), (), s32[]{:S(2)}) async-start(), calls=%async_computation | async-start | bytes 1327104 | tf_op jit(solution)/shard_map/all_gather | solution.py:75
  7.3 46.0 %copy-start.3 = (s32[16,32]{1,0:T(8,128)S(1)}, s32[16,32]{1,0:T(8,128)}, u32[]{:S(2)}) copy-start(s32[16,32]{1,0:T(8,128)} %param.6) | copy-start | bytes 6148
  37.7 13.3 %collective-permute-start = (f32[16,32,256]{2,1,0:T(8,128)S(1)}, f32[16,32,256]{2,1,0:T(8,128)S(1)}, u32[]{:S(2)}, u32[]{:S(2)}) collective-permute-start(f32[16,32,256]{2,1,0:T(8,128)S(1)} %fusion), channel_id=1, source_target_pairs={{0,1},{1,0},{2,3},{3,2},{4,5},{5,4},{6,7},{7,6},{8,9},{9,8},{10,11... | collective-permute-start | bytes 1572872 | tf_op jit(solution)/shard_map/ppermute | solution.py:81
  51.1 25.1 %collective-permute-start.1 = (f32[16,32,256]{2,1,0:T(8,128)S(1)}, f32[16,32,256]{2,1,0:T(8,128)S(1)}, u32[]{:S(2)}, u32[]{:S(2)}) collective-permute-start(f32[16,32,256]{2,1,0:T(8,128)S(1)} %add.291), channel_id=1, source_target_pairs={{0,2},{1,3},{2,0},{3,1},{4,6},{5,7},{6,4},{7,5},{8,10},{9,11},{10,... | collective-permute-start | bytes 1572872 | tf_op jit(solution)/shard_map/ppermute | solution.py:81
  53.3 6.3 %collective-permute-start.2 = (f32[3,32]{1,0:T(4,128)S(1)}, f32[3,32]{1,0:T(4,128)S(1)}, u32[]{:S(2)}, u32[]{:S(2)}) collective-permute-start(f32[3,32]{1,0:T(4,128)S(1)} %get-tuple-element.121), channel_id=1, source_target_pairs={{0,8},{8,16},{16,24},{1,9},{9,17},{17,25},{2,10},{10,18},{18,26},{... | collective-permute-start | bytes 1160 | tf_op jit(solution)/shard_map/ppermute | solution.py:17
  57.7 4.9 %collective-permute-start.3 = (f32[3,32]{1,0:T(4,128)S(1)}, f32[3,32]{1,0:T(4,128)S(1)}, u32[]{:S(2)}, u32[]{:S(2)}) collective-permute-start(f32[3,32]{1,0:T(4,128)S(1)} %get-tuple-element.122), channel_id=1, source_target_pairs={{8,0},{16,8},{24,16},{9,1},{17,9},{25,17},{10,2},{18,10},{26,18},{... | collective-permute-start | bytes 1160 | tf_op jit(solution)/shard_map/ppermute | solution.py:18
  76.3 11.7 %collective-permute-start.5 = (f32[3,32,256]{2,1,0:T(8,128)S(1)}, f32[3,32,256]{2,1,0:T(8,128)S(1)}, u32[]{:S(2)}, u32[]{:S(2)}) collective-permute-start(f32[3,32,256]{2,1,0:T(8,128)S(1)} %get-tuple-element.115), channel_id=1, source_target_pairs={{0,8},{8,16},{16,24},{1,9},{9,17},{17,25},{2,10},{10,18},{18,26},{... | collective-permute-start | bytes 294920 | tf_op jit(solution)/shard_map/ppermute | solution.py:17
  80.7 7.3 %collective-permute-start.6 = (f32[3,32,256]{2,1,0:T(8,128)S(1)}, f32[3,32,256]{2,1,0:T(8,128)S(1)}, u32[]{:S(2)}, u32[]{:S(2)}) collective-permute-start(f32[3,32,256]{2,1,0:T(8,128)S(1)} %get-tuple-element.116), channel_id=1, source_target_pairs={{8,0},{16,8},{24,16},{9,1},{17,9},{25,17},{10,2},{18,10},{26,18},{... | collective-permute-start | bytes 294920 | tf_op jit(solution)/shard_map/ppermute | solution.py:18
  82.7 8.0 %collective-permute-start.8 = (f32[22,3]{1,0:T(8,128)S(1)}, f32[22,3]{1,0:T(8,128)S(1)}, u32[]{:S(2)}, u32[]{:S(2)}) collective-permute-start(f32[22,3]{1,0:T(8,128)S(1)} %get-tuple-element.119), channel_id=1, source_target_pairs={{4,0},{5,1},{6,2},{7,3},{12,8},{13,9},{14,10},{15,11},{20,16},{21,... | collective-permute-start | bytes 800 | tf_op jit(solution)/shard_map/ppermute | solution.py:18
  84.0 6.7 %collective-permute-start.4 = (f32[22,3]{1,0:T(8,128)S(1)}, f32[22,3]{1,0:T(8,128)S(1)}, u32[]{:S(2)}, u32[]{:S(2)}) collective-permute-start(f32[22,3]{1,0:T(8,128)S(1)} %get-tuple-element.120), channel_id=1, source_target_pairs={{0,4},{1,5},{2,6},{3,7},{8,12},{9,13},{10,14},{11,15},{16,20},{17,... | collective-permute-start | bytes 800 | tf_op jit(solution)/shard_map/ppermute | solution.py:17
  88.0 2.8 %collective-permute-start.7 = (f32[22,3,256]{2,1,0:T(4,128)S(1)}, f32[22,3,256]{2,1,0:T(4,128)S(1)}, u32[]{:S(2)}, u32[]{:S(2)}) collective-permute-start(f32[22,3,256]{2,1,0:T(4,128)S(1)} %get-tuple-element.113), channel_id=1, source_target_pairs={{0,4},{1,5},{2,6},{3,7},{8,12},{9,13},{10,14},{11,15},{16,20},{17,... | collective-permute-start | bytes 202760 | tf_op jit(solution)/shard_map/ppermute | solution.py:17
  89.3 5.3 %collective-permute-start.9 = (f32[22,3,256]{2,1,0:T(4,128)S(1)}, f32[22,3,256]{2,1,0:T(4,128)S(1)}, u32[]{:S(2)}, u32[]{:S(2)}) collective-permute-start(f32[22,3,256]{2,1,0:T(4,128)S(1)} %get-tuple-element.114), channel_id=1, source_target_pairs={{4,0},{5,1},{6,2},{7,3},{12,8},{13,9},{14,10},{15,11},{20,16},{21,... | collective-permute-start | bytes 202760 | tf_op jit(solution)/shard_map/ppermute | solution.py:18
  98.7 1.1 copy-start.2
  100.0 5.3 %copy-start.1 = (bf16[2304,256]{0,1:T(8,128)(2,1)S(1)}, bf16[2304,256]{0,1:T(8,128)(2,1)}, u32[]{:S(2)}) copy-start(bf16[2304,256]{0,1:T(8,128)(2,1)} %all-gather.2.cloned.1.call-done) | copy-start | bytes 3538948
Sparse Core Ops, SparseCore 0:
  9.2 26.3 all-gather.1
